TPU v7x, 32 devices: a whole 2x2x4 slice. The times are simulated.
32 devices in a mesh: dp: 16 (over z, x, core), tensor: 2 (over y).
Axes of the slice: x: 2, y: 2, z: 4, core: 2. Of those that a mesh axis runs over, the one named last changes fastest.
Arguments:
- grad_hidden: bfloat16 [2048, 14336], P('dp', 'tensor'), may hold values from -18 to 18
- gate: bfloat16 [2048, 14336], P('dp', 'tensor'), may hold values from -6 to 6
Outputs:
- factor: float32 [14336, 14336], P('tensor', 'dp')
All inputs are finite; a program needn't handle non-finite values.
Results may differ from a plain program's by a relative error of at most 0.0065.
Values may be sent and summed in bfloat16 or wider, within the bound.
No kernel may reach another device: no remote copies, remote signals or barrier semaphores. Data moves between devices by JAX's collectives and lax.ppermute only.
A program may use at most 128 MiB of HBM per device.

v0:
```python
import jax
import jax.numpy as jnp
from jax import lax
from jax.sharding import PartitionSpec as P

FF = 14336


def shards(grad_hidden, gate):
    up_grad = (grad_hidden.astype(jnp.float32) * jax.nn.silu(gate.astype(jnp.float32))).astype(
        jnp.bfloat16
    )
    tensor_count = lax.axis_size("tensor")
    data_count = lax.axis_size("dp")
    col_width = FF // data_count
    ratio = data_count // tensor_count
    data_index = lax.axis_index("dp")
    owner = data_index // ratio
    offset = data_index % ratio * col_width
    contract = (((0,), (0,)), ((), ()))
    total_tokens = up_grad.shape[0] * data_count
    rows_all = lax.all_gather(up_grad, "dp", axis=0, tiled=True)
    panel = lax.dynamic_slice_in_dim(rows_all, offset, col_width, 1)
    slices = lax.all_gather(panel, "tensor", axis=1, tiled=True)
    cols_all = lax.dynamic_slice_in_dim(slices, owner * col_width, col_width, 1)
    summed = lax.dot_general(rows_all, cols_all, contract, preferred_element_type=jnp.float32)
    return summed / total_tokens


def solution(mesh):
    return jax.shard_map(
        shards,
        mesh=mesh,
        in_specs=(P("dp", "tensor"), P("dp", "tensor")),
        out_specs=P("tensor", "dp"),
        check_vma=False,
    )
```

profile of v0, /device:TPU:0, one launch (start us, length us, event | category | flops | bytes accessed | tf_op | source)
XLA Modules:
  0.0 303.7 jit_solution(14807854129925651823)
XLA Ops:
  6.5 0.0 all-gather.3.cloned.1.call-start
  6.5 4.4 %fusion.5 = bf16[128,7168]{1,0:T(8,128)(2,1)} fusion(bf16[128,7168]{1,0:T(8,128)(2,1)} %param.3, bf16[128,7168]{1,0:T(8,128)(2,1)} %param.2), kind=kLoop, calls=%fused_computation.8 | loop fusion | flops 7340032 | bytes 5505024 | tf_op jit(solution)/shard_map/convert_element_type | solution.py:10
  10.9 0.0 all-gather.3.cloned.1.call-update
  11.0 0.0 all-gather.5.cloned.1.call-start
  11.0 151.1 %all-gather.3.cloned.1.call-done = bf16[2048,7168]{1,0:T(8,128)(2,1)} async-done(((bf16[128,7168]{1,0:T(8,128)(2,1)}), bf16[2048,7168]{1,0:T(8,128)(2,1)}) %all-gather.3.cloned.1.call-update) | async-done | bytes 29360144 | tf_op jit(solution)/shard_map/all_gather | solution.py:22
  162.1 4.2 %constant_dynamic-slice_fusion = bf16[2048,896]{1,0:T(8,128)(2,1)} fusion(bf16[2048,7168]{1,0:T(8,128)(2,1)} %all-gather.3.cloned.1.call-done, s32[]{:T(128)S(6)} %select_n.18), kind=kLoop, calls=%fused_computation.10 | loop fusion | bytes 7340036 | tf_op jit(solution)/shard_map/dynamic_slice | solution.py:23
  166.3 0.0 all-gather.5.cloned.1.call-update
  166.3 92.3 %all-gather.5.cloned.1.call-done = bf16[2048,1792]{1,0:T(8,128)(2,1)} async-done(((bf16[2048,896]{1,0:T(8,128)(2,1)}), bf16[2048,1792]{1,0:T(8,128)(2,1)}) %all-gather.5.cloned.1.call-update) | async-done | bytes 7340048 | tf_op jit(solution)/shard_map/all_gather | solution.py:24
  258.6 38.3 %convolution_multiply_fusion = f32[7168,896]{1,0:T(8,128)} fusion(bf16[2048,7168]{1,0:T(8,128)(2,1)} %all-gather.3.cloned.1.call-done, bf16[2048,1792]{1,0:T(8,128)(2,1)} %all-gather.5.cloned.1.call-done, s32[]{:T(128)S(6)} %select_n.20), kind=kOutput, calls=%fused_computation | convolution fusion | flops 26313097216 | bytes 58720260 | tf_op jit(solution)/shard_map/dot_general | solution.py:26
Async XLA Ops:
  6.5 155.6 %all-gather.3.cloned.1.call-start = ((), (), s32[]{:S(2)}) async-start(), calls=%async_computation | async-start | bytes 31195136 | tf_op jit(solution)/shard_map/all_gather | solution.py:22
  11.0 247.7 %all-gather.5.cloned.1.call-start = ((), (), s32[]{:S(2)}) async-start(), calls=%async_computation.1 | async-start | bytes 11010048 | tf_op jit(solution)/shard_map/all_gather | solution.py:24
Sparse Core Ops, SparseCore 0:
  11.1 150.9 all-gather.2
  166.4 92.1 all-gather.4
where the time goes:
time: 304 us
  waiting for transfers between devices  243 us (80%)
  matrix products  38.3 us (13%)
  between operations  13.4 us (4%)
  other arithmetic  4.39 us (1%)
  local copies, waits for them, and re-layouts  4.17 us (1%)
    all_gather x1, waiting for transfers between devices, shards(): rows_all = lax.all_gather(up_grad, 'dp', axis=0, tiled=True)  151 us
    all_gather x1, waiting for transfers between devices, shards(): slices = lax.all_gather(panel, 'tensor', axis=1, tiled=True)  92.3 us
    dot_general x1, matrix products, shards(): lax.dot_general(rows_all, cols_all, contract, preferred_element_type=jnp....  38.3 us
  transfers between devices with their start and end apart: 2, of which 2 were waited for; matrix products, arithmetic and copies ran while one was open for 0% of the time, Pallas kernels for 0%

commit v1 on v0

--- a/solution.py
+++ b/solution.py
@@ -19,7 +19,13 @@
     offset = data_index % ratio * col_width
     contract = (((0,), (0,)), ((), ()))
     total_tokens = up_grad.shape[0] * data_count
-    rows_all = lax.all_gather(up_grad, "dp", axis=0, tiled=True)
+    peers = lax.axis_size("dp")
+    held, blocks = (up_grad, [up_grad])
+    for _ in range(peers - 1):
+        held = lax.ppermute(held, "dp", [(i, (i + 1) % peers) for i in range(peers)])
+        blocks.insert(0, held)
+    line = jnp.concatenate(blocks, axis=0)
+    rows_all = jnp.roll(line, (lax.axis_index("dp") + 1) * up_grad.shape[0], axis=0)
     panel = lax.dynamic_slice_in_dim(rows_all, offset, col_width, 1)
     slices = lax.all_gather(panel, "tensor", axis=1, tiled=True)
     cols_all = lax.dynamic_slice_in_dim(slices, owner * col_width, col_width, 1)

time: 304 us -> 620 us (2.04)
  waiting for transfers between devices: 243 us -> 471 us
  local copies, waits for them, and re-layouts: 4.17 us -> 92.1 us
    ppermute x0 -> x15, waiting for transfers between devices: none -> 381 us  [shards(): lax.ppermute(held, 'dp', [(i, (i + 1) % peers) for i in range(peers)])]
    all_gather x1 -> x0, waiting for transfers between devices: 151 us -> none  [shards(): rows_all = lax.all_gather(up_grad, 'dp', axis=0, tiled=True)]
    unnamed x0 -> x83, local copies, waits for them, and re-layouts: none -> 84.5 us
  transfers between devices with their start and end apart: 2 -> 16, of which waited for: 2 -> 16; matrix products, arithmetic and copies ran while one was open for 0% -> 0% of each run, Pallas kernels for 0% -> 0%
where the time goes in v1:
time: 620 us; the launch traced here: 619 us
  waiting for transfers between devices  471 us (76%)
  local copies, waits for them, and re-layouts  92.1 us (15%)
  matrix products  38.4 us (6%)
  between operations  13.6 us (2%)
    ppermute x15, waiting for transfers between devices, shards(): lax.ppermute(held, 'dp', [(i, (i + 1) % peers) for i in range(peers)])  381 us
    all_gather x1, waiting for transfers between devices, shards(): slices = lax.all_gather(panel, 'tensor', axis=1, tiled=True)  90.1 us
    unnamed x83, local copies, waits for them, and re-layouts  84.5 us
    dot_general x1, matrix products, shards(): lax.dot_general(rows_all, cols_all, contract, preferred_element_type=jnp....  38.4 us
  transfers between devices with their start and end apart: 16, of which 16 were waited for; matrix products, arithmetic and copies ran while one was open for 0% of the time, Pallas kernels for 0%

profile of v1, /device:TPU:0, one launch (start us, length us, event | category | flops | bytes accessed | tf_op | source)
XLA Modules:
  0.0 618.9 jit_solution(17043810119950618780)
XLA Ops:
  6.5 3.2 fusion.10
  10.2 25.9 %collective-permute-done = bf16[128,7168]{1,0:T(8,128)(2,1)S(1)} collective-permute-done((bf16[128,7168]{1,0:T(8,128)(2,1)S(1)}, bf16[128,7168]{1,0:T(8,128)(2,1)S(1)}, u32[]{:S(2)}, u32[]{:S(2)}) %collective-permute-start) | collective-permute-done | bytes 1835040 | tf_op jit(solution)/shard_map/ppermute | solution.py:25
  37.4 25.3 %collective-permute-done.1 = bf16[128,7168]{1,0:T(8,128)(2,1)S(1)} collective-permute-done((bf16[128,7168]{1,0:T(8,128)(2,1)S(1)}, bf16[128,7168]{1,0:T(8,128)(2,1)S(1)}, u32[]{:S(2)}, u32[]{:S(2)}) %collective-permute-start.1) | collective-permute-done | bytes 1835040 | tf_op jit(solution)/shard_map/ppermute | solution.py:25
  64.0 25.3 %collective-permute-done.2 = bf16[128,7168]{1,0:T(8,128)(2,1)S(1)} collective-permute-done((bf16[128,7168]{1,0:T(8,128)(2,1)S(1)}, bf16[128,7168]{1,0:T(8,128)(2,1)S(1)}, u32[]{:S(2)}, u32[]{:S(2)}) %collective-permute-start.2) | collective-permute-done | bytes 1835040 | tf_op jit(solution)/shard_map/ppermute | solution.py:25
  90.6 25.3 %collective-permute-done.3 = bf16[128,7168]{1,0:T(8,128)(2,1)S(1)} collective-permute-done((bf16[128,7168]{1,0:T(8,128)(2,1)S(1)}, bf16[128,7168]{1,0:T(8,128)(2,1)S(1)}, u32[]{:S(2)}, u32[]{:S(2)}) %collective-permute-start.3) | collective-permute-done | bytes 1835040 | tf_op jit(solution)/shard_map/ppermute | solution.py:25
  117.2 25.3 %collective-permute-done.4 = bf16[128,7168]{1,0:T(8,128)(2,1)S(1)} collective-permute-done((bf16[128,7168]{1,0:T(8,128)(2,1)S(1)}, bf16[128,7168]{1,0:T(8,128)(2,1)S(1)}, u32[]{:S(2)}, u32[]{:S(2)}) %collective-permute-start.4) | collective-permute-done | bytes 1835040 | tf_op jit(solution)/shard_map/ppermute | solution.py:25
  143.8 25.3 %collective-permute-done.5 = bf16[128,7168]{1,0:T(8,128)(2,1)S(1)} collective-permute-done((bf16[128,7168]{1,0:T(8,128)(2,1)S(1)}, bf16[128,7168]{1,0:T(8,128)(2,1)S(1)}, u32[]{:S(2)}, u32[]{:S(2)}) %collective-permute-start.5) | collective-permute-done | bytes 1835040 | tf_op jit(solution)/shard_map/ppermute | solution.py:25
  170.4 25.3 %collective-permute-done.6 = bf16[128,7168]{1,0:T(8,128)(2,1)S(1)} collective-permute-done((bf16[128,7168]{1,0:T(8,128)(2,1)S(1)}, bf16[128,7168]{1,0:T(8,128)(2,1)S(1)}, u32[]{:S(2)}, u32[]{:S(2)}) %collective-permute-start.6) | collective-permute-done | bytes 1835040 | tf_op jit(solution)/shard_map/ppermute | solution.py:25
  197.0 25.3 %collective-permute-done.7 = bf16[128,7168]{1,0:T(8,128)(2,1)S(1)} collective-permute-done((bf16[128,7168]{1,0:T(8,128)(2,1)S(1)}, bf16[128,7168]{1,0:T(8,128)(2,1)S(1)}, u32[]{:S(2)}, u32[]{:S(2)}) %collective-permute-start.7) | collective-permute-done | bytes 1835040 | tf_op jit(solution)/shard_map/ppermute | solution.py:25
  223.6 25.3 %collective-permute-done.8 = bf16[128,7168]{1,0:T(8,128)(2,1)S(1)} collective-permute-done((bf16[128,7168]{1,0:T(8,128)(2,1)S(1)}, bf16[128,7168]{1,0:T(8,128)(2,1)S(1)}, u32[]{:S(2)}, u32[]{:S(2)}) %collective-permute-start.8) | collective-permute-done | bytes 1835040 | tf_op jit(solution)/shard_map/ppermute | solution.py:25
  250.3 25.3 %collective-permute-done.9 = bf16[128,7168]{1,0:T(8,128)(2,1)S(1)} collective-permute-done((bf16[128,7168]{1,0:T(8,128)(2,1)S(1)}, bf16[128,7168]{1,0:T(8,128)(2,1)S(1)}, u32[]{:S(2)}, u32[]{:S(2)}) %collective-permute-start.9) | collective-permute-done | bytes 1835040 | tf_op jit(solution)/shard_map/ppermute | solution.py:25
  276.8 25.3 %collective-permute-done.10 = bf16[128,7168]{1,0:T(8,128)(2,1)S(1)} collective-permute-done((bf16[128,7168]{1,0:T(8,128)(2,1)S(1)}, bf16[128,7168]{1,0:T(8,128)(2,1)S(1)}, u32[]{:S(2)}, u32[]{:S(2)}) %collective-permute-start.10) | collective-permute-done | bytes 1835040 | tf_op jit(solution)/shard_map/ppermute | solution.py:25
  303.4 25.3 %collective-permute-done.11 = bf16[128,7168]{1,0:T(8,128)(2,1)S(1)} collective-permute-done((bf16[128,7168]{1,0:T(8,128)(2,1)S(1)}, bf16[128,7168]{1,0:T(8,128)(2,1)S(1)}, u32[]{:S(2)}, u32[]{:S(2)}) %collective-permute-start.11) | collective-permute-done | bytes 1835040 | tf_op jit(solution)/shard_map/ppermute | solution.py:25
  330.1 25.3 %collective-permute-done.12 = bf16[128,7168]{1,0:T(8,128)(2,1)S(1)} collective-permute-done((bf16[128,7168]{1,0:T(8,128)(2,1)S(1)}, bf16[128,7168]{1,0:T(8,128)(2,1)S(1)}, u32[]{:S(2)}, u32[]{:S(2)}) %collective-permute-start.12) | collective-permute-done | bytes 1835040 | tf_op jit(solution)/shard_map/ppermute | solution.py:25
  356.7 25.4 %collective-permute-done.13 = bf16[128,7168]{1,0:T(8,128)(2,1)} collective-permute-done((bf16[128,7168]{1,0:T(8,128)(2,1)S(1)}, bf16[128,7168]{1,0:T(8,128)(2,1)}, u32[]{:S(2)}, u32[]{:S(2)}) %collective-permute-start.13) | collective-permute-done | bytes 1835040 | tf_op jit(solution)/shard_map/ppermute | solution.py:25
  382.2 25.6 %collective-permute-done.14 = bf16[128,7168]{1,0:T(8,128)(2,1)} collective-permute-done((bf16[128,7168]{1,0:T(8,128)(2,1)}, bf16[128,7168]{1,0:T(8,128)(2,1)}, u32[]{:S(2)}, u32[]{:S(2)}) %collective-permute-start.14) | collective-permute-done | bytes 1835040 | tf_op jit(solution)/shard_map/ppermute | solution.py:25
  407.8 2.9 constant_dynamic-update-slice_fusion.31
  410.6 2.9 constant_dynamic-update-slice_fusion.30
  413.5 2.9 constant_dynamic-update-slice_fusion.29
  416.4 2.9 constant_dynamic-update-slice_fusion.28
  419.2 3.0 constant_dynamic-update-slice_fusion.27
  422.2 2.8 constant_dynamic-update-slice_fusion.26
  425.0 2.9 constant_dynamic-update-slice_fusion.25
  428.0 2.8 constant_dynamic-update-slice_fusion.24
  430.8 2.9 constant_dynamic-update-slice_fusion.23
  433.7 2.9 constant_dynamic-update-slice_fusion.22
  436.5 2.8 constant_dynamic-update-slice_fusion.21
  439.4 2.9 constant_dynamic-update-slice_fusion.20
  442.2 2.9 constant_dynamic-update-slice_fusion.19
  445.1 2.9 constant_dynamic-update-slice_fusion.18
  448.0 2.8 constant_dynamic-update-slice_fusion.17
  450.9 1.4 constant_dynamic-update-slice_fusion.16
  452.3 2.8 constant_dynamic-update-slice_fusion.15
  455.1 2.8 constant_dynamic-update-slice_fusion.14
  458.0 1.4 constant_dynamic-update-slice_fusion.13
  459.3 1.4 constant_dynamic-update-slice_fusion.12
  460.7 1.4 constant_dynamic-update-slice_fusion.11
  462.1 1.4 constant_dynamic-update-slice_fusion.10
  463.5 1.4 constant_dynamic-update-slice_fusion.9
  464.9 1.4 constant_dynamic-update-slice_fusion.8
  467.6 1.4 constant_dynamic-update-slice_fusion.6
  469.0 1.4 constant_dynamic-update-slice_fusion.5
  473.1 1.4 constant_dynamic-update-slice_fusion.2
  474.5 1.4 constant_dynamic-update-slice_fusion.1
  475.9 1.4 constant_dynamic-update-slice_fusion
  477.3 6.2 %dynamic_slice.11 = bf16[2048,896]{1,0:T(8,128)(2,1)} dynamic-slice(bf16[4096,7168]{1,0:T(8,128)(2,1)} %constant_dynamic-update-slice_fusion, s32[]{:T(128)S(6)} %select_n.35, s32[]{:T(128)S(6)} %select_n.38), dynamic_slice_sizes={2048,896} | dynamic-slice | bytes 7340036 | tf_op jit(solution)/shard_map/dynamic_slice | solution.py:29
  483.6 90.1 %all-gather.2.cloned.1.call-done = bf16[2048,1792]{1,0:T(8,128)(2,1)} async-done(((bf16[2048,896]{1,0:T(8,128)(2,1)}), bf16[2048,1792]{1,0:T(8,128)(2,1)}) %all-gather.2.cloned.1.call-update) | async-done | bytes 7340048 | tf_op jit(solution)/shard_map/all_gather | solution.py:30
  573.6 38.4 %fusion.2 = f32[7168,896]{1,0:T(8,128)} fusion(bf16[4096,7168]{1,0:T(8,128)(2,1)} %constant_dynamic-update-slice_fusion, s32[]{:T(128)S(6)} %select_n.34, bf16[2048,1792]{1,0:T(8,128)(2,1)} %all-gather.2.cloned.1.call-done, s32[]{:T(128)S(6)} %select_n.40), kind=kOutput, calls=%fused_computation.2 | convolution fusion | flops 26313097216 | bytes 58720264 | tf_op jit(solution)/shard_map/dot_general | solution.py:32
  (72 shorter events, 21.1 us)
Async XLA Ops:
  6.5 567.1 %all-gather.2.cloned.1.call-start = ((), (), s32[]{:S(2)}) async-start(), calls=%async_computation | async-start | bytes 11010048 | tf_op jit(solution)/shard_map/all_gather | solution.py:30
  9.7 26.4 %collective-permute-start = (bf16[128,7168]{1,0:T(8,128)(2,1)S(1)}, bf16[128,7168]{1,0:T(8,128)(2,1)S(1)}, u32[]{:S(2)}, u32[]{:S(2)}) collective-permute-start(bf16[128,7168]{1,0:T(8,128)(2,1)S(1)} %fusion.10), channel_id=1, source_target_pairs={{0,2},{2,4},{4,6},{6,8},{8,10},{10,12},{12,14},{14,16},{16,18},{18... | collective-permute-start | bytes 5505032 | tf_op jit(solution)/shard_map/ppermute | solution.py:25
  36.1 1.3 copy-start
  37.4 25.3 %collective-permute-start.1 = (bf16[128,7168]{1,0:T(8,128)(2,1)S(1)}, bf16[128,7168]{1,0:T(8,128)(2,1)S(1)}, u32[]{:S(2)}, u32[]{:S(2)}) collective-permute-start(bf16[128,7168]{1,0:T(8,128)(2,1)S(1)} %collective-permute-done), channel_id=1, source_target_pairs={{0,2},{2,4},{4,6},{6,8},{8,10},{10,12},{12,14},{14,16},{16,18},{18... | collective-permute-start | bytes 5505032 | tf_op jit(solution)/shard_map/ppermute | solution.py:25
  62.7 1.2 copy-start.2
  64.0 25.3 %collective-permute-start.2 = (bf16[128,7168]{1,0:T(8,128)(2,1)S(1)}, bf16[128,7168]{1,0:T(8,128)(2,1)S(1)}, u32[]{:S(2)}, u32[]{:S(2)}) collective-permute-start(bf16[128,7168]{1,0:T(8,128)(2,1)S(1)} %collective-permute-done.1), channel_id=1, source_target_pairs={{0,2},{2,4},{4,6},{6,8},{8,10},{10,12},{12,14},{14,16},{16,18},{18... | collective-permute-start | bytes 5505032 | tf_op jit(solution)/shard_map/ppermute | solution.py:25
  89.3 1.3 copy-start.4
  90.6 25.3 %collective-permute-start.3 = (bf16[128,7168]{1,0:T(8,128)(2,1)S(1)}, bf16[128,7168]{1,0:T(8,128)(2,1)S(1)}, u32[]{:S(2)}, u32[]{:S(2)}) collective-permute-start(bf16[128,7168]{1,0:T(8,128)(2,1)S(1)} %collective-permute-done.2), channel_id=1, source_target_pairs={{0,2},{2,4},{4,6},{6,8},{8,10},{10,12},{12,14},{14,16},{16,18},{18... | collective-permute-start | bytes 5505032 | tf_op jit(solution)/shard_map/ppermute | solution.py:25
  115.9 1.2 copy-start.6
  117.2 25.3 %collective-permute-start.4 = (bf16[128,7168]{1,0:T(8,128)(2,1)S(1)}, bf16[128,7168]{1,0:T(8,128)(2,1)S(1)}, u32[]{:S(2)}, u32[]{:S(2)}) collective-permute-start(bf16[128,7168]{1,0:T(8,128)(2,1)S(1)} %collective-permute-done.3), channel_id=1, source_target_pairs={{0,2},{2,4},{4,6},{6,8},{8,10},{10,12},{12,14},{14,16},{16,18},{18... | collective-permute-start | bytes 5505032 | tf_op jit(solution)/shard_map/ppermute | solution.py:25
  142.5 1.3 copy-start.8
  143.8 25.3 %collective-permute-start.5 = (bf16[128,7168]{1,0:T(8,128)(2,1)S(1)}, bf16[128,7168]{1,0:T(8,128)(2,1)S(1)}, u32[]{:S(2)}, u32[]{:S(2)}) collective-permute-start(bf16[128,7168]{1,0:T(8,128)(2,1)S(1)} %collective-permute-done.4), channel_id=1, source_target_pairs={{0,2},{2,4},{4,6},{6,8},{8,10},{10,12},{12,14},{14,16},{16,18},{18... | collective-permute-start | bytes 5505032 | tf_op jit(solution)/shard_map/ppermute | solution.py:25
  169.1 1.2 copy-start.10
  170.4 25.3 %collective-permute-start.6 = (bf16[128,7168]{1,0:T(8,128)(2,1)S(1)}, bf16[128,7168]{1,0:T(8,128)(2,1)S(1)}, u32[]{:S(2)}, u32[]{:S(2)}) collective-permute-start(bf16[128,7168]{1,0:T(8,128)(2,1)S(1)} %collective-permute-done.5), channel_id=1, source_target_pairs={{0,2},{2,4},{4,6},{6,8},{8,10},{10,12},{12,14},{14,16},{16,18},{18... | collective-permute-start | bytes 5505032 | tf_op jit(solution)/shard_map/ppermute | solution.py:25
  195.7 1.3 copy-start.12
  197.0 25.3 %collective-permute-start.7 = (bf16[128,7168]{1,0:T(8,128)(2,1)S(1)}, bf16[128,7168]{1,0:T(8,128)(2,1)S(1)}, u32[]{:S(2)}, u32[]{:S(2)}) collective-permute-start(bf16[128,7168]{1,0:T(8,128)(2,1)S(1)} %collective-permute-done.6), channel_id=1, source_target_pairs={{0,2},{2,4},{4,6},{6,8},{8,10},{10,12},{12,14},{14,16},{16,18},{18... | collective-permute-start | bytes 5505032 | tf_op jit(solution)/shard_map/ppermute | solution.py:25
  222.3 1.3 copy-start.14
  223.6 25.3 %collective-permute-start.8 = (bf16[128,7168]{1,0:T(8,128)(2,1)S(1)}, bf16[128,7168]{1,0:T(8,128)(2,1)S(1)}, u32[]{:S(2)}, u32[]{:S(2)}) collective-permute-start(bf16[128,7168]{1,0:T(8,128)(2,1)S(1)} %collective-permute-done.7), channel_id=1, source_target_pairs={{0,2},{2,4},{4,6},{6,8},{8,10},{10,12},{12,14},{14,16},{16,18},{18... | collective-permute-start | bytes 5505032 | tf_op jit(solution)/shard_map/ppermute | solution.py:25
  249.0 1.3 copy-start.16
  250.3 25.3 %collective-permute-start.9 = (bf16[128,7168]{1,0:T(8,128)(2,1)S(1)}, bf16[128,7168]{1,0:T(8,128)(2,1)S(1)}, u32[]{:S(2)}, u32[]{:S(2)}) collective-permute-start(bf16[128,7168]{1,0:T(8,128)(2,1)S(1)} %collective-permute-done.8), channel_id=1, source_target_pairs={{0,2},{2,4},{4,6},{6,8},{8,10},{10,12},{12,14},{14,16},{16,18},{18... | collective-permute-start | bytes 5505032 | tf_op jit(solution)/shard_map/ppermute | solution.py:25
  275.6 1.2 copy-start.18
  276.8 25.3 %collective-permute-start.10 = (bf16[128,7168]{1,0:T(8,128)(2,1)S(1)}, bf16[128,7168]{1,0:T(8,128)(2,1)S(1)}, u32[]{:S(2)}, u32[]{:S(2)}) collective-permute-start(bf16[128,7168]{1,0:T(8,128)(2,1)S(1)} %collective-permute-done.9), channel_id=1, source_target_pairs={{0,2},{2,4},{4,6},{6,8},{8,10},{10,12},{12,14},{14,16},{16,18},{18... | collective-permute-start | bytes 5505032 | tf_op jit(solution)/shard_map/ppermute | solution.py:25
  302.2 1.3 copy-start.20
  303.4 25.3 %collective-permute-start.11 = (bf16[128,7168]{1,0:T(8,128)(2,1)S(1)}, bf16[128,7168]{1,0:T(8,128)(2,1)S(1)}, u32[]{:S(2)}, u32[]{:S(2)}) collective-permute-start(bf16[128,7168]{1,0:T(8,128)(2,1)S(1)} %collective-permute-done.10), channel_id=1, source_target_pairs={{0,2},{2,4},{4,6},{6,8},{8,10},{10,12},{12,14},{14,16},{16,18},{18... | collective-permute-start | bytes 5505032 | tf_op jit(solution)/shard_map/ppermute | solution.py:25
  328.8 1.3 copy-start.22
  330.1 25.3 %collective-permute-start.12 = (bf16[128,7168]{1,0:T(8,128)(2,1)S(1)}, bf16[128,7168]{1,0:T(8,128)(2,1)S(1)}, u32[]{:S(2)}, u32[]{:S(2)}) collective-permute-start(bf16[128,7168]{1,0:T(8,128)(2,1)S(1)} %collective-permute-done.11), channel_id=1, source_target_pairs={{0,2},{2,4},{4,6},{6,8},{8,10},{10,12},{12,14},{14,16},{16,18},{18... | collective-permute-start | bytes 5505032 | tf_op jit(solution)/shard_map/ppermute | solution.py:25
  355.4 1.2 copy-start.24
  356.7 25.5 %collective-permute-start.13 = (bf16[128,7168]{1,0:T(8,128)(2,1)S(1)}, bf16[128,7168]{1,0:T(8,128)(2,1)}, u32[]{:S(2)}, u32[]{:S(2)}) collective-permute-start(bf16[128,7168]{1,0:T(8,128)(2,1)S(1)} %collective-permute-done.12), channel_id=1, source_target_pairs={{0,2},{2,4},{4,6},{6,8},{8,10},{10,12},{12,14},{14,16},{16,18},{18... | collective-permute-start | bytes 5505032 | tf_op jit(solution)/shard_map/ppermute | solution.py:25
  382.1 25.7 %collective-permute-start.14 = (bf16[128,7168]{1,0:T(8,128)(2,1)}, bf16[128,7168]{1,0:T(8,128)(2,1)}, u32[]{:S(2)}, u32[]{:S(2)}) collective-permute-start(bf16[128,7168]{1,0:T(8,128)(2,1)} %collective-permute-done.13), channel_id=1, source_target_pairs={{0,2},{2,4},{4,6},{6,8},{8,10},{10,12},{12,14},{14,16},{16,18},{18... | collective-permute-start | bytes 5505032 | tf_op jit(solution)/shard_map/ppermute | solution.py:25
  382.1 75.8 %copy-start.25 = (bf16[128,7168]{1,0:T(8,128)(2,1)S(1)}, bf16[128,7168]{1,0:T(8,128)(2,1)}, u32[]{:S(2)}) copy-start(bf16[128,7168]{1,0:T(8,128)(2,1)} %copy-done.24) | copy-start | bytes 5505028
  382.1 77.2 %copy-start.23 = (bf16[128,7168]{1,0:T(8,128)(2,1)S(1)}, bf16[128,7168]{1,0:T(8,128)(2,1)}, u32[]{:S(2)}) copy-start(bf16[128,7168]{1,0:T(8,128)(2,1)} %copy-done.22) | copy-start | bytes 5505028
  382.1 78.6 %copy-start.21 = (bf16[128,7168]{1,0:T(8,128)(2,1)S(1)}, bf16[128,7168]{1,0:T(8,128)(2,1)}, u32[]{:S(2)}) copy-start(bf16[128,7168]{1,0:T(8,128)(2,1)} %copy-done.20) | copy-start | bytes 5505028
  382.1 80.0 %copy-start.19 = (bf16[128,7168]{1,0:T(8,128)(2,1)S(1)}, bf16[128,7168]{1,0:T(8,128)(2,1)}, u32[]{:S(2)}) copy-start(bf16[128,7168]{1,0:T(8,128)(2,1)} %copy-done.18) | copy-start | bytes 5505028
  382.1 81.3 %copy-start.17 = (bf16[128,7168]{1,0:T(8,128)(2,1)S(1)}, bf16[128,7168]{1,0:T(8,128)(2,1)}, u32[]{:S(2)}) copy-start(bf16[128,7168]{1,0:T(8,128)(2,1)} %copy-done.16) | copy-start | bytes 5505028
  382.1 82.7 %copy-start.15 = (bf16[128,7168]{1,0:T(8,128)(2,1)S(1)}, bf16[128,7168]{1,0:T(8,128)(2,1)}, u32[]{:S(2)}) copy-start(bf16[128,7168]{1,0:T(8,128)(2,1)} %copy-done.14) | copy-start | bytes 5505028
  382.1 84.1 %copy-start.13 = (bf16[128,7168]{1,0:T(8,128)(2,1)S(1)}, bf16[128,7168]{1,0:T(8,128)(2,1)}, u32[]{:S(2)}) copy-start(bf16[128,7168]{1,0:T(8,128)(2,1)} %copy-done.12) | copy-start | bytes 5505028
  382.2 85.5 %copy-start.11 = (bf16[128,7168]{1,0:T(8,128)(2,1)S(1)}, bf16[128,7168]{1,0:T(8,128)(2,1)}, u32[]{:S(2)}) copy-start(bf16[128,7168]{1,0:T(8,128)(2,1)} %copy-done.10) | copy-start | bytes 5505028
  382.2 86.9 %copy-start.9 = (bf16[128,7168]{1,0:T(8,128)(2,1)S(1)}, bf16[128,7168]{1,0:T(8,128)(2,1)}, u32[]{:S(2)}) copy-start(bf16[128,7168]{1,0:T(8,128)(2,1)} %copy-done.8) | copy-start | bytes 5505028
  382.2 88.2 %copy-start.7 = (bf16[128,7168]{1,0:T(8,128)(2,1)S(1)}, bf16[128,7168]{1,0:T(8,128)(2,1)}, u32[]{:S(2)}) copy-start(bf16[128,7168]{1,0:T(8,128)(2,1)} %copy-done.6) | copy-start | bytes 5505028
  382.2 89.6 %copy-start.5 = (bf16[128,7168]{1,0:T(8,128)(2,1)S(1)}, bf16[128,7168]{1,0:T(8,128)(2,1)}, u32[]{:S(2)}) copy-start(bf16[128,7168]{1,0:T(8,128)(2,1)} %copy-done.4) | copy-start | bytes 5505028
  382.2 90.9 %copy-start.3 = (bf16[128,7168]{1,0:T(8,128)(2,1)S(1)}, bf16[128,7168]{1,0:T(8,128)(2,1)}, u32[]{:S(2)}) copy-start(bf16[128,7168]{1,0:T(8,128)(2,1)} %copy-done.2) | copy-start | bytes 5505028
  382.2 92.3 %copy-start.1 = (bf16[128,7168]{1,0:T(8,128)(2,1)S(1)}, bf16[128,7168]{1,0:T(8,128)(2,1)}, u32[]{:S(2)}) copy-start(bf16[128,7168]{1,0:T(8,128)(2,1)} %copy-done) | copy-start | bytes 5505028
Sparse Core Ops, SparseCore 0:
  483.7 89.9 all-gather.1
